TPU v7x, 32 devices: a 4x4x1 block of a 4x4x8 slice. The times are simulated.
32 devices in a mesh: dp: 1 (over z), tp: 32 (over x, y, core).
Axes of the slice: x: 4, y: 4, z: 1, core: 2. Of those that a mesh axis runs over, the one named last changes fastest.
The devices are a block of a 4x4x8 slice.
Arguments:
- x: bfloat16 [2048, 8192], P('dp')
- w_gate: bfloat16 [8192, 32768], P(None, 'tp')
- w_up: bfloat16 [8192, 32768], P(None, 'tp')
- w_down: bfloat16 [32768, 8192], P('tp')
Outputs:
- output: bfloat16 [2048, 8192], P('dp')
All inputs are finite; a program needn't handle non-finite values.
Results may differ from a plain program's by a relative error of at most 0.016.
Values are sent between devices in bfloat16 or wider.
A program may use at most 768 MiB of HBM per device.

v0:
```python
import jax
import jax.numpy as jnp
from jax import lax
from jax.sharding import PartitionSpec as P


def solution(mesh):
    def step(x, w_gate, w_up, w_down):
        gate = jnp.dot(x, w_gate, preferred_element_type=jnp.float32)
        up = jnp.dot(x, w_up, preferred_element_type=jnp.float32)
        hidden = (jax.nn.silu(gate) * up).astype(jnp.bfloat16)
        term = jnp.dot(hidden, w_down, preferred_element_type=jnp.float32).astype(jnp.bfloat16)
        return lax.psum(term, "tp")

    return jax.shard_map(
        step,
        mesh=mesh,
        in_specs=(P("dp", None), P(None, "tp"), P(None, "tp"), P("tp", None)),
        out_specs=P("dp", None),
        check_vma=False,
    )
```

profile of v0, /device:TPU:97, one launch (start us, length us, event | category | flops | bytes accessed | tf_op | source)
XLA Modules:
  0.0 423.8 jit_solution(18349792540878314891)
XLA Ops:
  6.5 0.0 all-reduce.2.cloned.1.call-start
  6.6 43.6 %fusion = f32[2048,1024]{1,0:T(8,128)} fusion(bf16[2048,8192]{1,0:T(8,128)(2,1)} %param.4, bf16[8192,1024]{1,0:T(8,128)(2,1)} %param.5), kind=kOutput, calls=%fused_computation.2 | convolution fusion | flops 34359738368 | bytes 58720256 | tf_op jit(solution)/shard_map/dot_general | solution.py:9
  50.2 45.4 %multiply_convert_fusion = bf16[2048,1024]{1,0:T(8,128)(2,1)} fusion(f32[2048,1024]{1,0:T(8,128)} %fusion, bf16[2048,8192]{1,0:T(8,128)(2,1)} %param.4, bf16[8192,1024]{1,0:T(8,128)(2,1)} %param.6), kind=kOutput, calls=%fused_computation.1 | convolution fusion | flops 34372321280 | bytes 62914560 | tf_op jit(solution)/shard_map/dot_general | solution.py:10
  95.6 44.9 %convolution_convert_fusion = bf16[2048,8192]{1,0:T(8,128)(2,1)} fusion(bf16[2048,1024]{1,0:T(8,128)(2,1)} %multiply_convert_fusion, bf16[1024,8192]{1,0:T(8,128)(2,1)} %param.7), kind=kOutput, calls=%fused_computation | convolution fusion | flops 34376515584 | bytes 54525952 | tf_op jit(solution)/shard_map/dot_general | solution.py:12
  140.5 0.1 all-reduce.2.cloned.1.call-update
  140.6 253.3 %all-reduce.2.cloned.1.call-done = bf16[2048,8192]{1,0:T(8,128)(2,1)} async-done(((bf16[2048,8192]{1,0:T(8,128)(2,1)}), bf16[2048,8192]{1,0:T(8,128)(2,1)}) %all-reduce.2.cloned.1.call-update) | async-done | bytes 33554448 | tf_op jit(solution)/shard_map/psum | solution.py:13
  393.9 23.0 %copy.6 = bf16[2048,8192]{1,0:T(8,128)(2,1)} copy(bf16[2048,8192]{1,0:T(8,128)(2,1)} %all-reduce.2.cloned.1.call-done) | data formatting | bytes 67108864
Async XLA Ops:
  6.5 387.4 %all-reduce.2.cloned.1.call-start = ((), (), s32[]{:S(2)}) async-start(), calls=%async_computation | async-start | bytes 67108864 | tf_op jit(solution)/shard_map/psum | solution.py:13
Sparse Core Ops, SparseCore 0:
  140.7 253.1 all-reduce.1
where the time goes:
time: 424 us
  waiting for transfers between devices  253 us (60%)
  matrix products  134 us (32%)
  local copies, waits for them, and re-layouts  23 us (5%)
  between operations  13.4 us (3%)
    psum x1, waiting for transfers between devices, step(): return lax.psum(term, 'tp')  253 us
    dot_general x1, matrix products, step(): up = jnp.dot(x, w_up, preferred_element_type=jnp.float32)  45.4 us
    dot_general x1, matrix products, step(): jnp.dot(hidden, w_down, preferred_element_type=jnp.float32)  44.9 us
    dot_general x1, matrix products, step(): gate = jnp.dot(x, w_gate, preferred_element_type=jnp.float32)  43.6 us
    unnamed x1, local copies, waits for them, and re-layouts  23 us
  transfers between devices with their start and end apart: 1, of which 1 were waited for; matrix products, arithmetic and copies ran while one was open for 0% of the time, Pallas kernels for 0%

commit v1 on v0

v1 whole, which is shorter than its diff:
```python
import math

import jax
import jax.numpy as jnp
from jax import lax
from jax.experimental import pallas as pl
from jax.experimental.pallas import tpu as pltpu
from jax.sharding import PartitionSpec as P

MESH = pl.DeviceIdType.MESH
ROWS = 256
NT = 256
SIDE = 4
WD_SLOTS = 4
D_SLOTS = 3
STEPS = 12
POS = {
    "S1": [13, 25, 37, 49, 61, 74, 86, 97],
    "S2": [20, 32, 44, 56, 69, 81, 94, 101],
    "S3": [23, 35, 47, 60, 74, 86, 98, 105],
    "S4": [25, 39, 50, 62, 86, 94, 102, 108],
    "S5": [27, 45, 60, 69, 89, 99, 106, 111],
    "S6": [33, 49, 63, 74, 96, 103, 109, 113],
    "S7": [46, 60, 73, 85, 100, 107, 112, 115],
    "S8": [50, 70, 82, 94, 104, 110, 114, 116],
}
N_STEPS = 117
POS_BACK = 112


def _kernel(
    x_hbm, wg_hbm, wu_hbm, wd_hbm, y_hbm, wv,
    xv, hv, wd, acc, dsend, drecv,
    s1a, r1a, s1b, r1b, own, s2a, r2a, s2b, r2b, fin,
    x_sem, w_sem, wd_sem, d_ss, d_rs,
    s1a_ss, s1a_rs, s1b_ss, s1b_rs, s2a_ss, s2a_rs, s2b_ss, s2b_rs,
    fin_sem, g2a_ss, g2a_rs, g2b_ss, g2b_rs, g1a_ss, g1a_rs, g1b_ss, g1b_rs,
    dd_ss, dd_rs, credit, back_sem,
):
    chunks = x_hbm.shape[0] // ROWS
    cols = y_hbm.shape[1]
    half = cols // 2
    pc = half // SIDE
    nt = hv.shape[1] // NT
    first = chunks // 2
    up_rows = first * ROWS
    last = chunks - 1
    ph = ROWS // 2
    hp = ph // 2
    sr = ph // SIDE
    hs = sr // 2

    me = lax.axis_index("tp")
    core = lax.rem(me, 2)
    yi = lax.rem(me // 2, SIDE)
    xi = me // (2 * SIDE)

    def dev(a, b, c):
        return {"tp": (a * SIDE + b) * 2 + c}

    def mod(v):
        return lax.rem(v + 2 * SIDE, SIDE)

    partner = dev(xi, yi, 1 - core)
    x_nxt, x_prv = dev(mod(xi + 1), yi, core), dev(mod(xi - 1), yi, core)
    y_nxt, y_prv = dev(xi, mod(yi + 1), core), dev(xi, mod(yi - 1), core)
    me1, me2 = (xi, yi), (yi, xi)
    to1 = ((x_nxt, x_prv), (y_nxt, y_prv))
    to2 = ((y_nxt, y_prv), (x_nxt, x_prv))

    barrier = pltpu.get_barrier_semaphore()
    for d in (partner, x_nxt, x_prv, y_nxt, y_prv):
        pl.semaphore_signal(barrier, inc=1, device_id=d, device_id_type=MESH)

    def rcopy(src, dst, ss, rs, to):
        return pltpu.make_async_remote_copy(
            src_ref=src, dst_ref=dst, send_sem=ss, recv_sem=rs, device_id=to, device_id_type=MESH
        )

    def x_copy(t):
        return pltpu.make_async_copy(x_hbm.at[pl.ds(t * ROWS, ROWS), :], xv, x_sem)

    def w_tile(n, at, width):
        return wv.at[n // 2, :, pl.ds(pl.multiple_of((n % 2) * 2 * NT + at, NT), width)]

    def w_copies(n):
        c = pl.ds(n * NT, NT)
        return (
            pltpu.make_async_copy(wg_hbm.at[:, c], w_tile(n, 0, NT), w_sem.at[n, 0]),
            pltpu.make_async_copy(wu_hbm.at[:, c], w_tile(n, NT, NT), w_sem.at[n, 1]),
        )

    fx, fy = mod(xi + 2), mod(yi + 2)
    e = mod(fy - fx)
    o1 = jnp.maximum(e, 1)
    o2 = jnp.where(o1 == 1, 2, 1)
    o3 = jnp.where(o1 == 3, 2, 3)

    def piece_at(i):
        o = jnp.where(i == 0, 0, jnp.where(i == 1, o1, jnp.where(i == 2, o2, o3)))
        return mod(fx + o)

    def wd_copy(j):
        mine = j // SIDE
        hc = mine * core + (1 - mine) * (1 - core)
        c = pl.multiple_of(hc * half + piece_at(lax.rem(j, SIDE)) * pc, pc)
        s = lax.rem(j, WD_SLOTS)
        return pltpu.make_async_copy(wd_hbm.at[:, pl.ds(c, pc)], wd.at[s], wd_sem.at[s])

    x_copy(0).start()
    for n in range(nt):
        for c in w_copies(n):
            c.start()
    for j in range(WD_SLOTS):
        wd_copy(jnp.int32(j)).start()

    pl.semaphore_wait(barrier, 5)

    f32, bf16 = jnp.float32, jnp.bfloat16

    def gate_up(t, n):
        @pl.when(n == 0)
        def _():
            x_copy(t).wait()

        @pl.when(t == 0)
        def _():
            for c in w_copies(n):
                c.wait()

        for m in range(nt):
            @pl.when(n == m)
            def _():
                w = wv[m // 2, :, (m % 2) * 2 * NT : (m % 2 + 1) * 2 * NT]
                gu = jnp.dot(xv[...], w, preferred_element_type=f32)
                g, u = gu[:, :NT], gu[:, NT:]
                hv[:, m * NT : (m + 1) * NT] = (jax.nn.silu(g) * u).astype(bf16)

        @pl.when((n == nt - 1) & (t < last))
        def _():
            x_copy(t + 1).start()

        @pl.when((n == nt // 2 - 1) & (t == last))
        def _():
            for d in (partner, x_nxt, x_prv, y_nxt, y_prv):
                pl.semaphore_signal(credit, inc=1, device_id=d, device_id_type=MESH)

    def d_copy(t, q, n=0):
        s, m = lax.rem(t, 2), n % D_SLOTS
        return rcopy(dsend.at[m], drecv.at[s, q], d_ss.at[m], d_rs.at[s, q], partner)

    def down(t, j):
        s = lax.rem(j, WD_SLOTS)
        q = piece_at(lax.rem(j, SIDE))
        wd_copy(j).wait()

        @pl.when(j < SIDE)
        def _():
            n = t * SIDE + j

            @pl.when(n >= D_SLOTS)
            def _():
                d_copy(t, q, n).wait_send()

            r = jnp.dot(hv[...], wd[s], preferred_element_type=f32)
            dsend[lax.rem(n, D_SLOTS)] = r.astype(bf16)
            d_copy(t, q, n).start()

        @pl.when(j >= SIDE)
        def _():
            d_copy(t, q).wait_recv()
            r = jnp.dot(hv[...], wd[s], preferred_element_type=f32)
            acc[q] = r + drecv[lax.rem(t, 2), q].astype(f32)

        @pl.when(j < SIDE)
        def _():
            wd_copy(j + SIDE).start()

        @pl.when((j >= SIDE) & (t < last))
        def _():
            wd_copy(j - SIDE).start()

        @pl.when(j == SIDE + 1)
        def _():
            S0(t)

    hd = [(h, d) for h in range(2) for d in range(2)]

    def c1a(k, h, d):
        s = lax.rem(k, 2)
        return rcopy(s1a.at[h, d], r1a.at[s, h, d], s1a_ss.at[h, d], s1a_rs.at[s, h, d], to1[h][d])

    def c1b(k, h, d):
        s = lax.rem(k, 2)
        return rcopy(s1b.at[h, d], r1b.at[s, h, d], s1b_ss.at[h, d], s1b_rs.at[s, h, d], to1[h][d])

    def c2a(k, h, d):
        s = lax.rem(k, 2)
        return rcopy(s2a.at[h, d], r2a.at[s, h, d], s2a_ss.at[h, d], s2a_rs.at[s, h, d], to2[h][d])

    def c2b(k, h, d):
        s = lax.rem(k, 2)
        return rcopy(s2b.at[h, d], r2b.at[s, h, d], s2b_ss.at[h, d], s2b_rs.at[s, h, d], to2[h][d])

    def sent(copy, k, *a):
        @pl.when(k > 0)
        def _():
            copy(k - 1, *a).wait_send()

    def S0(k):
        s = lax.rem(k, 2)
        for h, d in hd:
            sent(c1a, k, h, d)
            far = mod(me1[h] + 2)
            s1a[h, d] = acc[far, pl.ds(h * ph + d * hp, hp), :].astype(bf16)
            c1a(k, h, d).start()

    def S1(k):
        s = lax.rem(k, 2)
        for h in range(2):
            own[s, h] = acc[me1[h], pl.ds(h * ph, ph), :]
        for h, d in hd:
            sent(c1b, k, h, d)
            c1a(k, h, d).wait_recv()
            near = mod(me1[h] + (1, -1)[d])
            other = 1 - d
            s1b[h, d, pl.ds(d * hp, hp), :] = (
                acc[near, pl.ds(h * ph + d * hp, hp), :] + r1a[s, h, d].astype(f32)
            ).astype(bf16)
            s1b[h, d, pl.ds(other * hp, hp), :] = acc[
                near, pl.ds(h * ph + other * hp, hp), :
            ].astype(bf16)
            c1b(k, h, d).start()

    def S2(k):
        s = lax.rem(k, 2)
        for h in range(2):
            for d in range(2):
                c1b(k, h, d).wait_recv()
            own[s, h] = (
                own[s, h]
                + r1b[s, h, 0].astype(f32)
                + r1b[s, h, 1].astype(f32)
            )
            far = mod(me2[h] + 2)
            for d in range(2):
                sent(c2a, k, h, d)
                r0 = pl.multiple_of(far * sr + d * hs, hs)
                s2a[h, d] = own[s, h, pl.ds(r0, hs), :].astype(bf16)
                c2a(k, h, d).start()

    def S3(k):
        s = lax.rem(k, 2)
        for h, d in hd:
            sent(c2b, k, h, d)
            c2a(k, h, d).wait_recv()
            near = mod(me2[h] + (1, -1)[d])
            other = 1 - d
            r0 = pl.multiple_of(near * sr + d * hs, hs)
            r1 = pl.multiple_of(near * sr + other * hs, hs)
            s2b[h, d, pl.ds(d * hs, hs), :] = (
                own[s, h, pl.ds(r0, hs), :] + r2a[s, h, d].astype(f32)
            ).astype(bf16)
            s2b[h, d, pl.ds(other * hs, hs), :] = own[s, h, pl.ds(r1, hs), :].astype(bf16)
            c2b(k, h, d).start()

    def region(k, vm, h, piece, r0, rows):
        p = core * SIDE + piece
        if vm:
            a = pl.multiple_of(p * up_rows + (k - first) * ROWS + h * ph + r0, 16)
            return wv.at[0, pl.ds(a, rows), :]
        a = pl.multiple_of(k * ROWS + h * ph + r0, 16)
        return y_hbm.at[pl.ds(a, rows), pl.ds(pl.multiple_of(p * pc, pc), pc)]

    def fin_local(k, h):
        s = lax.rem(k, 2)
        return pltpu.make_async_copy(
            fin.at[s, h], region(k, False, h, me1[h], me2[h] * sr, sr), fin_sem.at[s, h]
        )

    def g2a(k, vm, h, d):
        s = lax.rem(k, 2)
        return rcopy(
            fin.at[s, h], region(k, vm, h, me1[h], me2[h] * sr, sr),
            g2a_ss.at[s, h, d], g2a_rs.at[k, h, d], to2[h][d],
        )

    def g2b(k, vm, h, d):
        s = lax.rem(k, 2)
        src = mod(me2[h] - (1, -1)[d])
        r = region(k, vm, h, me1[h], src * sr + d * hs, hs)
        return rcopy(r, r, g2b_ss.at[s, h, d], g2b_rs.at[k, h, d], to2[h][d])

    def g1a(k, vm, h, d):
        s = lax.rem(k, 2)
        r = region(k, vm, h, me1[h], 0, ph)
        return rcopy(r, r, g1a_ss.at[s, h, d], g1a_rs.at[k, h, d], to1[h][d])

    def g1b(k, vm, h, d):
        s = lax.rem(k, 2)
        src = mod(me1[h] - (1, -1)[d])
        r = region(k, vm, h, src, d * hp, hp)
        return rcopy(r, r, g1b_ss.at[s, h, d], g1b_rs.at[k, h, d], to1[h][d])

    def dd(k, vm, h, o):
        s = lax.rem(k, 2)
        r = region(k, vm, h, mod(me1[h] + o), 0, ph)
        return rcopy(r, r, dd_ss.at[s, h, o], dd_rs.at[k, h, o], partner)

    def before(copy, k, vm, *a):
        @pl.when(k >= 2)
        def _():
            copy(k, vm, *a).wait_send()

    def S4(k, vm):
        s = lax.rem(k, 2)
        if vm:
            @pl.when(k == first)
            def _():
                pl.semaphore_wait(credit, 5)

        for h in range(2):
            for d in range(2):
                c2b(k, h, d).wait_recv()
                before(g2a, k, vm, h, d)
            r0 = pl.multiple_of(me2[h] * sr, sr)
            v = (
                own[s, h, pl.ds(r0, sr), :] + r2b[s, h, 0].astype(f32) + r2b[s, h, 1].astype(f32)
            ).astype(bf16)
            fin[s, h] = v
            if vm:
                a = pl.multiple_of(
                    (core * SIDE + me1[h]) * up_rows + (k - first) * ROWS + h * ph + me2[h] * sr, sr
                )
                wv[0, pl.ds(a, sr), :] = v
            for d in range(2):
                g2a(k, vm, h, d).start()
            if not vm:
                fin_local(k, h).start()

    def S5(k, vm):
        for h, d in hd:
            g2a(k, vm, h, d).wait_recv()
            before(g2b, k, vm, h, d)
            g2b(k, vm, h, d).start()
        if not vm:
            for h in range(2):
                fin_local(k, h).wait()

    def S6(k, vm):
        for h in range(2):
            for d in range(2):
                g2b(k, vm, h, d).wait_recv()
            for d in range(2):
                before(g1a, k, vm, h, d)
                g1a(k, vm, h, d).start()

    def S7(k, vm):
        for h, d in hd:
            g1a(k, vm, h, d).wait_recv()
            before(g1b, k, vm, h, d)
            g1b(k, vm, h, d).start()
        for h in range(2):
            for o in (0, 1, 3):
                before(dd, k, vm, h, o)
                dd(k, vm, h, o).start()

    def S8(k, vm):
        for h, d in hd:
            g1b(k, vm, h, d).wait_recv()
        for h in range(2):
            before(dd, k, vm, h, 2)
            dd(k, vm, h, 2).start()

    ho = [(h, o) for h in range(2) for o in range(4)]

    def back(p):
        return pltpu.make_async_copy(
            y_hbm.at[:, pl.ds(p * pc, pc)], wv.at[1, pl.ds(p * up_rows, up_rows), :], back_sem.at[p]
        )

    reduce = dict(S1=S1, S2=S2, S3=S3)
    gather = dict(S4=S4, S5=S5, S6=S6, S7=S7, S8=S8)

    @pl.loop(0, N_STEPS)
    def _(step):
        t, i = step // STEPS, lax.rem(step, STEPS)

        @pl.when((t < chunks) & (i < nt))
        def _():
            gate_up(t, i)

        @pl.when((t < chunks) & (i >= nt))
        def _():
            down(t, i - nt)

        for name in ("S2", "S4", "S1", "S3", "S5", "S6", "S7", "S8"):
            at = POS[name]
            assert len(at) == chunks
            hit = step == at[0]
            k = jnp.int32(0)
            for p in at[1:]:
                hit = hit | (step == p)
            for p in at:
                k = k + jnp.where(step > p, 1, 0)
            if name in reduce:
                @pl.when(hit)
                def _():
                    reduce[name](k)
            else:
                @pl.when(hit & (k < first))
                def _():
                    gather[name](k, False)

                @pl.when(hit & (k >= first))
                def _():
                    gather[name](k, True)

        @pl.when(step == POS_BACK)
        def _():
            @pl.loop(0, first)
            def _(k):
                for h, o in ho:
                    dd(k, False, h, o).wait_recv()

            for p in range(2 * SIDE):
                back(p).start()

    for p in range(2 * SIDE):
        back(p).wait()
    for k in range(first, chunks):
        for h, o in ho:
            dd(k, True, h, o).wait_recv()
    for n in range(D_SLOTS):
        d_copy(last, 0, n).wait_send()
    for f in (c1a, c1b, c2a, c2b):
        for h, d in hd:
            f(last, h, d).wait_send()
    for k in (last - 1, last):
        for f in (g2a, g2b, g1a, g1b):
            for h, d in hd:
                f(k, True, h, d).wait_send()
        for h, o in ho:
            dd(k, True, h, o).wait_send()


def _write(v_ref, y_ref, sem):
    pieces = y_ref.shape[1] // v_ref.shape[2]
    rows = v_ref.shape[1] // pieces
    copies = []
    for g in range(2):
        for p in range(pieces):
            src = v_ref.at[1 - g, pl.ds(p * rows, rows), :]
            dst = y_ref.at[pl.ds(g * rows, rows), pl.ds(p * v_ref.shape[2], v_ref.shape[2])]
            copies.append(pltpu.make_async_copy(src, dst, sem.at[g, p]))
    for c in copies:
        c.start()
    for c in copies:
        c.wait()


def solution(mesh):
    def step(x, w_gate, w_up, w_down):
        rows, depth = x.shape
        hidden = w_gate.shape[1]
        cols = w_down.shape[1]
        chunks = rows // ROWS
        pc = cols // 2 // SIDE
        ph = ROWS // 2
        sr = ph // SIDE
        assert mesh.shape["tp"] == 2 * SIDE * SIDE
        assert depth == cols and SIDE * rows == depth and hidden == 4 * NT == pc
        bf16, f32 = jnp.bfloat16, jnp.float32
        dma = pltpu.SemaphoreType.DMA
        V = pltpu.VMEM
        _, v = pl.pallas_call(
            _kernel,
            out_shape=(
                jax.ShapeDtypeStruct((rows // 2, cols), bf16),
                pltpu.VMEM((2, depth, pc), bf16),
            ),
            in_specs=[pl.BlockSpec(memory_space=pl.ANY)] * 4,
            out_specs=(
                pl.BlockSpec(memory_space=pl.ANY),
                pl.BlockSpec(memory_space=pltpu.VMEM),
            ),
            scratch_shapes=[
                V((ROWS, depth), bf16),
                V((ROWS, hidden), bf16),
                V((WD_SLOTS, hidden, pc), bf16),
                V((SIDE, ROWS, pc), f32),
                V((D_SLOTS, ROWS, pc), bf16),
                V((2, SIDE, ROWS, pc), bf16),
                V((2, 2, ph // 2, pc), bf16),
                V((2, 2, 2, ph // 2, pc), bf16),
                V((2, 2, ph, pc), bf16),
                V((2, 2, 2, ph, pc), bf16),
                V((2, 2, ph, pc), f32),
                V((2, 2, sr // 2, pc), bf16),
                V((2, 2, 2, sr // 2, pc), bf16),
                V((2, 2, sr, pc), bf16),
                V((2, 2, 2, sr, pc), bf16),
                V((2, 2, sr, pc), bf16),
                dma, dma((hidden // NT, 2)), dma((WD_SLOTS,)), dma((D_SLOTS,)), dma((2, SIDE)),
                dma((2, 2)), dma((2, 2, 2)), dma((2, 2)), dma((2, 2, 2)),
                dma((2, 2)), dma((2, 2, 2)), dma((2, 2)), dma((2, 2, 2)),
                dma((2, 2)),
                dma((2, 2, 2)), dma((chunks, 2, 2)), dma((2, 2, 2)), dma((chunks, 2, 2)),
                dma((2, 2, 2)), dma((chunks, 2, 2)), dma((2, 2, 2)), dma((chunks, 2, 2)),
                dma((2, 2, SIDE)), dma((chunks, 2, SIDE)),
                pltpu.SemaphoreType.REGULAR, dma((2 * SIDE,)),
            ],
            compiler_params=pltpu.CompilerParams(
                collective_id=0, has_side_effects=True, vmem_limit_bytes=67043328 - 4 * depth * pc
            ),
            cost_estimate=pl.CostEstimate(
                flops=6 * rows * depth * hidden, bytes_accessed=0, transcendentals=0
            ),
        )(x, w_gate, w_up, w_down)

        return pl.pallas_call(
            _write,
            out_shape=jax.ShapeDtypeStruct((rows, cols), bf16),
            in_specs=[pl.BlockSpec(memory_space=pltpu.VMEM)],
            out_specs=pl.BlockSpec(memory_space=pl.ANY),
            scratch_shapes=[dma((2, 2 * SIDE))],
            compiler_params=pltpu.CompilerParams(vmem_limit_bytes=2**22),
        )(pltpu.with_memory_space_constraint(v, pltpu.VMEM))

    return jax.shard_map(
        step,
        mesh=mesh,
        in_specs=(P("dp", None), P(None, "tp"), P(None, "tp"), P("tp", None)),
        out_specs=P("dp", None),
        check_vma=False,
    )
```

time: 424 us -> 243 us (0.57)
  waiting for transfers between devices: 253 us -> 0 us
  Pallas kernels: 0 us -> 243 us
  matrix products: 134 us -> 0 us
  local copies, waits for them, and re-layouts: 23 us -> 0 us
  between operations: 13.4 us -> 0.01 us
    psum x1 -> x0, waiting for transfers between devices: 253 us -> none  [step(): return lax.psum(term, 'tp')]
    pallas_call x0 -> x2, Pallas kernels: none -> 243 us  [the longest x1 232 us: step(): pl.pallas_call(_kernel, out_shape=(jax.ShapeDtypeStruct((rows // 2, cols)...]
    dot_general x3 -> x0, matrix products: 134 us -> none  [the longest x1 45.4 us: step(): up = jnp.dot(x, w_up, preferred_element_type=jnp.float32)]
    unnamed x1 -> x0, local copies, waits for them, and re-layouts: 23 us -> none
  transfers between devices with their start and end apart: 1 -> 0, of which waited for: 1 -> 0; matrix products, arithmetic and copies ran while one was open for 0% -> 0% of each run, Pallas kernels for 0% -> 0%
where the time goes in v1:
time: 243 us
  Pallas kernels  243 us (100%)
    pallas_call x1, Pallas kernels, step(): pl.pallas_call(_kernel, out_shape=(jax.ShapeDtypeStruct((rows // 2, cols)...  232 us
    pallas_call x1, Pallas kernels, step(): pl.pallas_call(_write, out_shape=jax.ShapeDtypeStruct((rows, cols), bf16)...  11 us

profile of v1, /device:TPU:97, one launch (start us, length us, event | category | flops | bytes accessed | tf_op | source)
XLA Modules:
  0.0 242.7 jit_solution(6439207777420066252)
XLA Ops:
  0.0 231.6 %shard_map.46 = (bf16[1024,8192]{1,0:T(8,128)(2,1)}, bf16[2,8192,1024]{2,1,0:T(8,128)(2,1)S(1)}) custom-call(bf16[2048,8192]{1,0:T(8,128)(2,1)} %x_hbm.1, bf16[8192,1024]{1,0:T(8,128)(2,1)} %wg_hbm.1, bf16[8192,1024]{1,0:T(8,128)(2,1)} %wu_hbm.1, bf16[1024,8192]{1,0:T(8,128)(2,1)} %wd_hbm.1), custom_call_target="tpu_custom_call" | custom-call | flops 103079215104 | tf_op jit(solution)/shard_map/pallas_call | solution.py:476
  231.6 11.0 %shard_map.47 = bf16[2048,8192]{1,0:T(8,128)(2,1)} custom-call(bf16[2,8192,1024]{2,1,0:T(8,128)(2,1)S(1)} %get-tuple-element.6.v_ref), custom_call_target="tpu_custom_call" | custom-call | tf_op jit(solution)/shard_map/pallas_call | solution.py:521

commit v2 on v1

--- a/solution.py
+++ b/solution.py
@@ -15,17 +15,17 @@
 D_SLOTS = 3
 STEPS = 12
 POS = {
-    "S1": [13, 25, 37, 49, 61, 74, 86, 97],
-    "S2": [20, 32, 44, 56, 69, 81, 94, 101],
-    "S3": [23, 35, 47, 60, 74, 86, 98, 105],
-    "S4": [25, 39, 50, 62, 86, 94, 102, 108],
-    "S5": [27, 45, 60, 69, 89, 99, 106, 111],
-    "S6": [33, 49, 63, 74, 96, 103, 109, 113],
-    "S7": [46, 60, 73, 85, 100, 107, 112, 115],
-    "S8": [50, 70, 82, 94, 104, 110, 114, 116],
+    "S1": [13, 25, 38, 52, 61, 72, 86, 101],
+    "S2": [16, 28, 44, 58, 69, 78, 91, 104],
+    "S3": [20, 34, 47, 61, 73, 84, 95, 106],
+    "S4": [24, 38, 50, 66, 86, 87, 103, 116],
+    "S5": [26, 41, 55, 71, 86, 101, 108, 120],
+    "S6": [31, 49, 62, 74, 88, 104, 116, 123],
+    "S7": [38, 53, 78, 80, 101, 114, 122, 131],
+    "S8": [56, 79, 103, 104, 108, 118, 123, 131],
 }
-N_STEPS = 117
-POS_BACK = 112
+N_STEPS = 132
+POS_BACK = 121
 
 
 def _kernel(
@@ -184,15 +184,25 @@
         def _():
             S0(t)
 
+        @pl.when(j == 2 * SIDE - 1)
+        def _():
+            S0b(t)
+
     hd = [(h, d) for h in range(2) for d in range(2)]
 
     def c1a(k, h, d):
         s = lax.rem(k, 2)
         return rcopy(s1a.at[h, d], r1a.at[s, h, d], s1a_ss.at[h, d], s1a_rs.at[s, h, d], to1[h][d])
 
-    def c1b(k, h, d):
-        s = lax.rem(k, 2)
-        return rcopy(s1b.at[h, d], r1b.at[s, h, d], s1b_ss.at[h, d], s1b_rs.at[s, h, d], to1[h][d])
+    def hrows(d, p):
+        return pl.ds((d if p == 0 else 1 - d) * hp, hp)
+
+    def c1b(k, h, d, p):
+        s, r = lax.rem(k, 2), hrows(d, p)
+        return rcopy(
+            s1b.at[h, d, r, :], r1b.at[s, h, d, r, :],
+            s1b_ss.at[h, d, p], s1b_rs.at[s, h, d, p], to1[h][d],
+        )
 
     def c2a(k, h, d):
         s = lax.rem(k, 2)
@@ -215,28 +225,32 @@
             s1a[h, d] = acc[far, pl.ds(h * ph + d * hp, hp), :].astype(bf16)
             c1a(k, h, d).start()
 
+    def S0b(k):
+        for h, d in hd:
+            sent(c1b, k, h, d, 1)
+            near = mod(me1[h] + (1, -1)[d])
+            s1b[h, d, hrows(d, 1), :] = acc[near, pl.ds(h * ph + (1 - d) * hp, hp), :].astype(bf16)
+            c1b(k, h, d, 1).start()
+
     def S1(k):
         s = lax.rem(k, 2)
+        for h, d in hd:
+            sent(c1b, k, h, d, 0)
+            c1a(k, h, d).wait_recv()
+            near = mod(me1[h] + (1, -1)[d])
+            s1b[h, d, hrows(d, 0), :] = (
+                acc[near, pl.ds(h * ph + d * hp, hp), :] + r1a[s, h, d].astype(f32)
+            ).astype(bf16)
+            c1b(k, h, d, 0).start()
         for h in range(2):
             own[s, h] = acc[me1[h], pl.ds(h * ph, ph), :]
-        for h, d in hd:
-            sent(c1b, k, h, d)
-            c1a(k, h, d).wait_recv()
-            near = mod(me1[h] + (1, -1)[d])
-            other = 1 - d
-            s1b[h, d, pl.ds(d * hp, hp), :] = (
-                acc[near, pl.ds(h * ph + d * hp, hp), :] + r1a[s, h, d].astype(f32)
-            ).astype(bf16)
-            s1b[h, d, pl.ds(other * hp, hp), :] = acc[
-                near, pl.ds(h * ph + other * hp, hp), :
-            ].astype(bf16)
-            c1b(k, h, d).start()
 
     def S2(k):
         s = lax.rem(k, 2)
         for h in range(2):
             for d in range(2):
-                c1b(k, h, d).wait_recv()
+                for p in range(2):
+                    c1b(k, h, d, p).wait_recv()
             own[s, h] = (
                 own[s, h]
                 + r1b[s, h, 0].astype(f32)
@@ -291,10 +305,10 @@
         r = region(k, vm, h, me1[h], src * sr + d * hs, hs)
         return rcopy(r, r, g2b_ss.at[s, h, d], g2b_rs.at[k, h, d], to2[h][d])
 
-    def g1a(k, vm, h, d):
-        s = lax.rem(k, 2)
-        r = region(k, vm, h, me1[h], 0, ph)
-        return rcopy(r, r, g1a_ss.at[s, h, d], g1a_rs.at[k, h, d], to1[h][d])
+    def g1a(k, vm, h, d, p):
+        s = lax.rem(k, 2)
+        r = region(k, vm, h, me1[h], (d if p == 0 else 1 - d) * hp, hp)
+        return rcopy(r, r, g1a_ss.at[s, h, d, p], g1a_rs.at[k, h, d, p], to1[h][d])
 
     def g1b(k, vm, h, d):
         s = lax.rem(k, 2)
@@ -348,24 +362,29 @@
                 fin_local(k, h).wait()
 
     def S6(k, vm):
-        for h in range(2):
-            for d in range(2):
-                g2b(k, vm, h, d).wait_recv()
-            for d in range(2):
-                before(g1a, k, vm, h, d)
-                g1a(k, vm, h, d).start()
+        for h, d in hd:
+            g2b(k, vm, h, d).wait_recv()
+        for p in range(2):
+            for h, d in hd:
+                before(g1a, k, vm, h, d, p)
+                g1a(k, vm, h, d, p).start()
 
     def S7(k, vm):
         for h, d in hd:
-            g1a(k, vm, h, d).wait_recv()
+            g1a(k, vm, h, d, 0).wait_recv()
             before(g1b, k, vm, h, d)
             g1b(k, vm, h, d).start()
         for h in range(2):
-            for o in (0, 1, 3):
+            before(dd, k, vm, h, 0)
+            dd(k, vm, h, 0).start()
+
+    def S8(k, vm):
+        for h, d in hd:
+            g1a(k, vm, h, d, 1).wait_recv()
+        for h in range(2):
+            for o in (1, 3):
                 before(dd, k, vm, h, o)
                 dd(k, vm, h, o).start()
-
-    def S8(k, vm):
         for h, d in hd:
             g1b(k, vm, h, d).wait_recv()
         for h in range(2):
@@ -433,13 +452,17 @@
             dd(k, True, h, o).wait_recv()
     for n in range(D_SLOTS):
         d_copy(last, 0, n).wait_send()
-    for f in (c1a, c1b, c2a, c2b):
-        for h, d in hd:
+    for h, d in hd:
+        for f in (c1a, c2a, c2b):
             f(last, h, d).wait_send()
+        for p in range(2):
+            c1b(last, h, d, p).wait_send()
     for k in (last - 1, last):
-        for f in (g2a, g2b, g1a, g1b):
-            for h, d in hd:
+        for h, d in hd:
+            for f in (g2a, g2b, g1b):
                 f(k, True, h, d).wait_send()
+            for p in range(2):
+                g1a(k, True, h, d, p).wait_send()
         for h, o in ho:
             dd(k, True, h, o).wait_send()
 
@@ -502,11 +525,11 @@
                 V((2, 2, 2, sr, pc), bf16),
                 V((2, 2, sr, pc), bf16),
                 dma, dma((hidden // NT, 2)), dma((WD_SLOTS,)), dma((D_SLOTS,)), dma((2, SIDE)),
-                dma((2, 2)), dma((2, 2, 2)), dma((2, 2)), dma((2, 2, 2)),
+                dma((2, 2)), dma((2, 2, 2)), dma((2, 2, 2)), dma((2, 2, 2, 2)),
                 dma((2, 2)), dma((2, 2, 2)), dma((2, 2)), dma((2, 2, 2)),
                 dma((2, 2)),
                 dma((2, 2, 2)), dma((chunks, 2, 2)), dma((2, 2, 2)), dma((chunks, 2, 2)),
-                dma((2, 2, 2)), dma((chunks, 2, 2)), dma((2, 2, 2)), dma((chunks, 2, 2)),
+                dma((2, 2, 2, 2)), dma((chunks, 2, 2, 2)), dma((2, 2, 2)), dma((chunks, 2, 2)),
                 dma((2, 2, SIDE)), dma((chunks, 2, SIDE)),
                 pltpu.SemaphoreType.REGULAR, dma((2 * SIDE,)),
             ],

time: 243 us -> 240 us (0.988)
  Pallas kernels: 243 us -> 239 us
    pallas_call x1, Pallas kernels: 232 us -> 228 us  [step(): pl.pallas_call(_kernel, out_shape=(jax.ShapeDtypeStruct((rows // 2, cols)...]
where the time goes in v2:
time: 240 us
  Pallas kernels  239 us (100%)
    pallas_call x1, Pallas kernels, step(): pl.pallas_call(_kernel, out_shape=(jax.ShapeDtypeStruct((rows // 2, cols)...  228 us
    pallas_call x1, Pallas kernels, step(): pl.pallas_call(_write, out_shape=jax.ShapeDtypeStruct((rows, cols), bf16)...  11 us

profile of v2, /device:TPU:97, one launch (start us, length us, event | category | flops | bytes accessed | tf_op | source)
XLA Modules:
  0.0 239.5 jit_solution(6978102674972074647)
XLA Ops:
  0.0 228.5 %shard_map.46 = (bf16[1024,8192]{1,0:T(8,128)(2,1)}, bf16[2,8192,1024]{2,1,0:T(8,128)(2,1)S(1)}) custom-call(bf16[2048,8192]{1,0:T(8,128)(2,1)} %x_hbm.1, bf16[8192,1024]{1,0:T(8,128)(2,1)} %wg_hbm.1, bf16[8192,1024]{1,0:T(8,128)(2,1)} %wu_hbm.1, bf16[1024,8192]{1,0:T(8,128)(2,1)} %wd_hbm.1), custom_call_target="tpu_custom_call" | custom-call | flops 103079215104 | tf_op jit(solution)/shard_map/pallas_call | solution.py:499
  228.5 11.0 %shard_map.47 = bf16[2048,8192]{1,0:T(8,128)(2,1)} custom-call(bf16[2,8192,1024]{2,1,0:T(8,128)(2,1)S(1)} %get-tuple-element.6.v_ref), custom_call_target="tpu_custom_call" | custom-call | tf_op jit(solution)/shard_map/pallas_call | solution.py:544
